TPU v7x, 128 devices: a whole 4x4x4 slice. The times are simulated.
128 devices in a mesh: col: 64 (over y_lo, z, x, core), row: 2 (over y_hi).
Axes of the slice: x: 4, y: 4 (y_hi: 2, y_lo: 2; y = y_hi * 2 + y_lo), z: 4, core: 2. Of those that a mesh axis runs over, the one named last changes fastest.
Arguments:
- matrix: float32 [8192, 8192], P('row', 'col'), as said below
- row_diag: float32 [2, 8192], P(None, 'row'), may hold values from 0.8 to 1.2
- col_diag: float32 [2, 8192], P(None, 'col'), may hold values from 0.8 to 1.2
Outputs:
- factored: float32 [8192, 8192], P('row', 'col')
Inputs may be any that keep to these rules, and one draw needn't show every extreme that they name: `matrix`: off the diagonal the entries lie within -6 and 6; the diagonal entries exceed 1.5 * sqrt(512) - 6.
All inputs are finite; a program needn't handle non-finite values.
Results may differ from a plain program's by a relative error of at most 0.0001.
Values sent between devices are 32-bit elements; how exact they have to be, the bound alone decides.
A program may use at most 64 MiB of HBM per device.

v0:
```python
import jax
import jax.numpy as jnp
from jax import lax
from jax.sharding import PartitionSpec as P

PW = 256
PANELS = 2


inv_root = 0.7071067811865476


def swapped(x, axis, distance):
    return lax.ppermute(x, axis, [(i, i ^ 1 << distance) for i in range(lax.axis_size(axis))])


def from_root(x, axis, root):
    mine = lax.axis_index(axis) == root
    return lax.psum(jnp.where(mine, x, jnp.zeros_like(x)), axis)


def picked(x, axis, root):
    return lax.dynamic_index_in_dim(lax.all_gather(x, axis), root, 0, keepdims=False)


def lu_block(block):
    size = block.shape[0]
    places = jnp.arange(size)

    def eliminate(step, current):
        pivot = current[step, step]
        below = places > step
        column = jnp.where(below, current[:, step] / pivot, 0.0)
        across = jnp.where(below, current[step, :], 0.0)
        current = current - column[:, None] * across[None, :]
        return jnp.where((places == step)[None, :] & below[:, None], column[:, None], current)

    return lax.fori_loop(0, size, eliminate, block)


def hdot(left, right):
    return jnp.dot(left, right, precision=lax.Precision.HIGHEST, preferred_element_type=jnp.float32)


def strict_inverse(strict):
    size = strict.shape[0]
    identity = jnp.eye(size, dtype=strict.dtype)
    result = identity - strict
    power = strict
    exponent = 1
    while exponent * 2 < size:
        power = hdot(power, power)
        exponent = exponent * 2
        result = hdot(result, identity + power)
    return result


def inverses(packed):
    upper_factor = jnp.triu(packed)
    lower_inverse = strict_inverse(jnp.tril(packed, -1))
    pivots = jnp.diagonal(packed)
    scaled = jnp.triu(packed, 1) / pivots[:, None]
    upper_inverse = strict_inverse(scaled) / pivots[None, :]
    return (lower_inverse, upper_inverse, upper_factor)


def pair_mix(own, partner, is_first, scales):
    return scales * jnp.where(is_first, own + partner, partner - own) * inv_root


def shards(matrix, row_diag, col_diag):
    height, width = matrix.shape
    row_pos = lax.axis_index("row")
    col_pos = lax.axis_index("col")
    first_row = row_pos * height
    first_col = col_pos * width
    rows = first_row + jnp.arange(height, dtype=jnp.int32)[:, None]
    cols = first_col + jnp.arange(width, dtype=jnp.int32)[None, :]
    partner = swapped(matrix, "row", 0)
    current = pair_mix(matrix, partner, row_pos == 0, row_diag[0][:, None])
    half = height // 2
    upper_part, lower_part = (current[:half], current[half:])
    current = jnp.concatenate(
        [
            row_diag[1][:half, None] * (upper_part + lower_part) * inv_root,
            row_diag[1][half:, None] * (upper_part - lower_part) * inv_root,
        ],
        0,
    )
    top_bit = lax.axis_size("col").bit_length() - 2
    partner = swapped(current, "col", top_bit)
    current = pair_mix(current, partner, col_pos // 2**top_bit % 2 == 0, col_diag[0][None, :])
    partner = swapped(current, "col", top_bit - 1)
    current = pair_mix(
        current, partner, col_pos // 2 ** (top_bit - 1) % 2 == 0, col_diag[1][None, :]
    )
    count = PW // width
    for panel in range(PANELS):
        start = panel * PW
        stop = start + PW
        owner = start // width
        offset = jnp.clip(start - first_row, 0, height - PW)
        band_local = lax.dynamic_slice_in_dim(current, offset, PW, 0)
        panel_parts = []
        for piece in range(count):
            panel_parts.append(from_root(current, "col", owner + piece))
        panel_block = jnp.concatenate(panel_parts, 1)
        diag_local = lax.dynamic_slice_in_dim(panel_block, offset, PW, 0)
        diag_block, band_rows = (picked(diag_local, "row", 0), picked(band_local, "row", 0))
        packed = lu_block(diag_block)
        lower_inverse, upper_inverse, upper_factor = inverses(packed)
        lower_rows = hdot(panel_block, upper_inverse)
        upper_cols = hdot(lower_inverse, band_rows)
        below = rows >= stop
        right = cols >= stop
        inside = (cols >= start) & (cols < stop)
        updated = current - hdot(
            jnp.where(below, lower_rows, 0.0), jnp.where(right, upper_cols, 0.0)
        )
        col_offset = jnp.clip(first_col - start, 0, PW - width)
        lower_cols = lax.dynamic_slice_in_dim(lower_rows, col_offset, width, 1)
        updated = jnp.where(below & inside, lower_cols, updated)
        packed_cols = lax.dynamic_slice_in_dim(packed, col_offset, width, 1)
        new_band = jnp.where(right, upper_cols, jnp.where(inside, packed_cols, band_rows))
        placed = lax.dynamic_update_slice_in_dim(updated, new_band, offset, 0)
        in_band = (rows >= start) & (rows < stop)
        current = jnp.where(in_band, placed, updated)
    return current


def solution(mesh):
    in_specs = (P("row", "col"), P(None, "row"), P(None, "col"))
    out_specs = P("row", "col")
    return jax.shard_map(shards, mesh=mesh, in_specs=in_specs, out_specs=out_specs, check_vma=False)
```

profile of v0, /device:TPU:6, one launch (start us, length us, event | category | flops | bytes accessed | tf_op | source)
XLA Modules:
  0.0 2178.8 jit_solution(17728124682734795352)
XLA Ops:
  6.5 3.2 collective-permute-start
  11.3 44.4 %collective-permute-done = f32[4096,128]{1,0:T(8,128)S(1)} collective-permute-done((f32[4096,128]{1,0:T(8,128)}, f32[4096,128]{1,0:T(8,128)S(1)}, u32[]{:S(2)}, u32[]{:S(2)}) %collective-permute-start) | collective-permute-done | bytes 2097184 | tf_op jit(solution)/shard_map/ppermute | solution.py:14
  55.6 1.9 multiply_multiply_fusion.2
  61.3 45.2 %collective-permute-done.1 = f32[4096,128]{1,0:T(8,128)} collective-permute-done((f32[4096,128]{1,0:T(8,128)}, f32[4096,128]{1,0:T(8,128)}, u32[]{:S(2)}, u32[]{:S(2)}) %collective-permute-start.1) | collective-permute-done | bytes 2097184 | tf_op jit(solution)/shard_map/ppermute | solution.py:14
  106.6 3.3 multiply_multiply_fusion.1
  109.8 3.9 collective-permute-start.2
  113.7 44.1 %collective-permute-done.2 = f32[4096,128]{1,0:T(8,128)S(1)} collective-permute-done((f32[4096,128]{1,0:T(8,128)}, f32[4096,128]{1,0:T(8,128)S(1)}, u32[]{:S(2)}, u32[]{:S(2)}) %collective-permute-start.2) | collective-permute-done | bytes 2097184 | tf_op jit(solution)/shard_map/ppermute | solution.py:14
  159.2 4.0 broadcast_select_fusion.2
  165.2 7.1 all-gather.1
  172.3 545.4 %all-reduce.7.cloned.1.call-done = (f32[4096,128]{1,0:T(8,128)}, f32[4096,128]{1,0:T(8,128)}) async-done(((f32[4096,128]{1,0:T(8,128)}, f32[4096,128]{1,0:T(8,128)}), (f32[4096,128]{1,0:T(8,128)}, f32[4096,128]{1,0:T(8,128)})) %all-reduce.7.cloned.1.call-update) | async-done | bytes 4194320 | tf_op jit(solution)/shard_map/psum | solution.py:19
  717.7 1.9 constant_dynamic-update-slice_fusion.1
  720.2 8.8 all-gather
  729.1 407.7 %while.30 = (s32[]{:T(128)}, f32[256,256]{0,1:T(8,128)S(1)}, s32[]{:T(128)}) while((s32[]{:T(128)}, f32[256,256]{0,1:T(8,128)S(1)}, s32[]{:T(128)}) %tuple.81), condition=%wide.region_3.4_spmd.clone.clone, body=%wide.region_2.3_spmd.clone.clone.sunk | while | flops 263426 | bytes 1056329 | solution.py:38
  1138.3 2.5 gather_fusion
  1150.5 3.9 fusion.84
  1155.2 3.6 fusion.5
  1160.1 2.3 broadcast_select_fusion
  1162.4 7.1 all-gather.3
  1169.6 557.7 %all-reduce.5.cloned.1.call-done = (f32[4096,128]{1,0:T(8,128)}, f32[4096,128]{1,0:T(8,128)}) async-done(((f32[4096,128]{1,0:T(8,128)}, f32[4096,128]{1,0:T(8,128)}), (f32[4096,128]{1,0:T(8,128)}, f32[4096,128]{1,0:T(8,128)})) %all-reduce.5.cloned.1.call-update) | async-done | bytes 4194320 | tf_op jit(solution)/shard_map/psum | solution.py:19
  1729.7 8.8 all-gather.2
  1738.7 407.7 %while.31 = (s32[]{:T(128)}, f32[256,256]{0,1:T(8,128)S(1)}, s32[]{:T(128)}) while((s32[]{:T(128)}, f32[256,256]{0,1:T(8,128)S(1)}, s32[]{:T(128)}) %tuple.84), condition=%wide.region_7.8_spmd.clone.clone, body=%wide.region_6.7_spmd.clone.clone.sunk | while | flops 263426 | bytes 1056329 | solution.py:38
  2147.8 2.8 gather_fusion.1
  2160.3 3.9 fusion.96
  2164.9 3.7 fusion.4
  (3188 shorter events, 828.1 us)
Async XLA Ops:
  6.5 711.2 %all-reduce.7.cloned.1.call-start = ((), (), s32[]{:S(2)}) async-start(), calls=%async_computation.1 | async-start | bytes 8388608 | tf_op jit(solution)/shard_map/psum | solution.py:19
  6.5 49.1 %collective-permute-start = (f32[4096,128]{1,0:T(8,128)}, f32[4096,128]{1,0:T(8,128)S(1)}, u32[]{:S(2)}, u32[]{:S(2)}) collective-permute-start(f32[4096,128]{1,0:T(8,128)} %param.7), channel_id=1, source_target_pairs={{0,1},{1,0},{2,3},{3,2},{4,5},{5,4},{6,7},{7,6},{8,9},{9,8},{10,11... | collective-permute-start | bytes 6291464 | tf_op jit(solution)/shard_map/ppermute | solution.py:14
  58.3 3.0 copy-start.10
  59.7 46.8 %collective-permute-start.1 = (f32[4096,128]{1,0:T(8,128)}, f32[4096,128]{1,0:T(8,128)}, u32[]{:S(2)}, u32[]{:S(2)}) collective-permute-start(f32[4096,128]{1,0:T(8,128)} %pad_maximum_fusion), channel_id=1, source_target_pairs={{0,64},{2,66},{4,68},{6,70},{8,72},{10,74},{12,76},{14,78},{16,80}... | collective-permute-start | bytes 6291464 | tf_op jit(solution)/shard_map/ppermute | solution.py:14
  109.8 48.0 %collective-permute-start.2 = (f32[4096,128]{1,0:T(8,128)}, f32[4096,128]{1,0:T(8,128)S(1)}, u32[]{:S(2)}, u32[]{:S(2)}) collective-permute-start(f32[4096,128]{1,0:T(8,128)} %multiply_multiply_fusion.1), channel_id=1, source_target_pairs={{0,32},{2,34},{4,36},{6,38},{8,40},{10,42},{12,44},{14,46},{16,48}... | collective-permute-start | bytes 6291464 | tf_op jit(solution)/shard_map/ppermute | solution.py:14
  157.8 1.3 copy-start.7
  163.1 2.0 copy-start
  164.7 1562.5 %all-reduce.5.cloned.1.call-start = ((), (), s32[]{:S(2)}) async-start(), calls=%async_computation | async-start | bytes 8388608 | tf_op jit(solution)/shard_map/psum | solution.py:19
  717.7 2.2 copy-start.8
  720.1 8.9 copy-start.2
  1148.1 2.4 copy-start.3
  1150.5 4.7 copy-start.1
  1727.3 2.2 copy-start.9
  1729.7 8.9 copy-start.4
  2157.9 2.4 copy-start.5
  2168.6 1.3 copy-start.6
Sparse Core Ops, SparseCore 0:
  164.9 552.8 all-reduce.6
  1162.5 564.7 all-reduce.4
where the time goes:
time: 2200 us; the launch traced here: 2180 us
  waiting for transfers between devices  1240 us (56%)
  other arithmetic  435 us (20%)
  local copies, waits for them, and re-layouts  387 us (18%)
  matrix products  38.1 us (2%)
  blocking collectives  31.9 us (1%)
  loops' own time  26.7 us (1%)
    psum x2, waiting for transfers between devices, from_root(): return lax.psum(jnp.where(mine, x, jnp.zeros_like(x)), axis)  1100 us
    select_n x512, other arithmetic, eliminate(): column = jnp.where(below, current[:, step] / pivot, 0.0)  335 us
    dynamic_slice x512, local copies, waits for them, and re-layouts, eliminate(): pivot = current[step, step]  303 us
    ppermute x3, waiting for transfers between devices, swapped(): lax.ppermute(x, axis, [(i, i ^ 1 << distance) for i in range(lax.axis_siz...  134 us
    select_n x512, other arithmetic, eliminate(): jnp.where((places == step)[None, :] & below[:, None], column[:, None], cu...  75.2 us
    while x512, local copies, waits for them, and re-layouts  65.8 us
  transfers between devices with their start and end apart: 5, of which 5 were waited for; matrix products, arithmetic and copies ran while one was open for 0% of the time, Pallas kernels for 0%

commit v1 on v0

v1 whole, which is shorter than its diff:
```python
import jax
import jax.numpy as jnp
from jax import lax
from jax.experimental import pallas as pl
from jax.experimental.pallas import tpu as pltpu
from jax.sharding import PartitionSpec as P

HI = lax.Precision.HIGHEST


def hdot(a, b):
    return jnp.dot(a, b, precision=HI, preferred_element_type=jnp.float32)


def rows_to(x, height):
    return jnp.broadcast_to(x, (height, x.shape[1]))


def lane_to(x, lane, width=128):
    return jnp.broadcast_to(x[:, lane : lane + 1], (x.shape[0], width))


def lu128(s, group=4):
    sub = lax.broadcasted_iota(jnp.int32, (8, 128), 0)
    lane = lax.broadcasted_iota(jnp.int32, (8, 128), 1)
    tiles = [s[8 * t : 8 * t + 8, :] for t in range(16)]
    extra = [jnp.where(lane == sub + 8 * t, 1.0, 0.0) for t in range(16)]
    packed = [None] * 16
    for b in range(16):
        rows, rows2 = tiles[b], extra[b]
        cols = [lane_to(rows, 8 * b + c) for c in range(8)]
        inv, ups, u = [], [], {}
        for c in range(8):
            r = 1.0 / rows_to(cols[c][c : c + 1], 8)
            inv.append(r)
            m = jnp.where(sub > c, cols[c] * r, 0.0)
            top = jnp.where(lane > 8 * b + c, rows_to(rows[c : c + 1], 8), 0.0)
            rows = jnp.where((lane == 8 * b + c) & (sub > c), m, rows - m * top)
            if c < 7:
                rows2 = rows2 - m * rows_to(rows2[c : c + 1], 8)
            for d in range(c + 1, 8):
                u[c, d] = rows_to(cols[d][c : c + 1], 8)
                cols[d] = cols[d] - m * u[c, d]
        packed[b] = rows
        extra[b] = rows2
        inside = (lane >= 8 * b) & (lane < 8 * b + 8)
        past = lane >= 8 * b + 8
        tiles[b] = jnp.where(lane == sub + 8 * b, 1.0, 0.0)
        ups = []
        for c in range(8):
            top = jnp.where(past, rows_to(rows[c : c + 1], 8), 0.0)
            ups.append(jnp.where(lane == 8 * b + c, -1.0, top))
        ups2 = [rows_to(rows2[c : c + 1], 8) for c in range(8)]
        order = list(range(b + 1, 16)) + list(range(b + 1))
        for t in order:
            tile = tiles[t]
            ls = [lane_to(tile, 8 * b + c) for c in range(8)]
            for c in range(8):
                ls[c] = ls[c] * inv[c]
                for d in range(c + 1, 8):
                    ls[d] = ls[d] - ls[c] * u[c, d]
            tile = jnp.where(inside, 0.0, tile)
            for c in range(8):
                tile = tile - ls[c] * ups[c]
            tiles[t] = tile
            if t > b:
                e = extra[t]
                for c in range(8):
                    e = e - ls[c] * ups2[c]
                extra[t] = e
    return packed, extra, tiles


def lu_kernel(a_ref, p_ref, li_ref, ui_ref):
    n = a_ref.shape[0]
    nb = n // 128
    ui_ref[...] = a_ref[...]
    ri = lax.broadcasted_iota(jnp.int32, (n, n), 0)
    ci = lax.broadcasted_iota(jnp.int32, (n, n), 1)
    li_ref[...] = jnp.where(ri == ci, 1.0, 0.0)

    def step(k, _):
        o = pl.multiple_of(k * 128, 128)
        blk = pl.ds(o, 128)
        packed, lower, upper = lu128(ui_ref[blk, blk])
        packed = jnp.concatenate(packed, 0)
        lower = jnp.concatenate(lower, 0)
        upper = jnp.concatenate(upper, 0)
        bc = lax.broadcasted_iota(jnp.int32, (128, n), 1)
        br = lax.broadcasted_iota(jnp.int32, (128, n), 0)
        band = ui_ref[blk, :]
        right = hdot(lower, band)
        p_ref[blk, :] = jnp.where(bc >= o + 128, right, band)
        p_ref[blk, blk] = packed
        right = jnp.where(bc >= o + 128, right, 0.0)
        ui_ref[blk, :] = jnp.where(bc == br + o, 1.0, 0.0)
        lband = hdot(lower, li_ref[blk, :])
        li_ref[blk, :] = lband
        left = hdot(ui_ref[:, blk], upper)
        ui_ref[...] = ui_ref[...] - hdot(left, right)
        ui_ref[:, blk] = left
        lr = lax.broadcasted_iota(jnp.int32, (n, 128), 0)
        li_ref[...] = li_ref[...] - hdot(jnp.where(lr >= o + 128, left, 0.0), lband)
        return 0

    lax.fori_loop(0, nb, step, 0)


MESH = pl.DeviceIdType.MESH
VMEM = pl.BlockSpec(memory_space=pltpu.VMEM)
inv_root = 0.7071067811865476


def place():
    r, c = lax.axis_index("row"), lax.axis_index("col")
    return r * 4 + c // 16, c % 16


def member(m, g):
    return {"row": m // 4, "col": (m % 4) * 16 + g}


def remote(src, dst, send, recv, device):
    return pltpu.make_async_remote_copy(
        src, dst, send, recv, device_id=device, device_id_type=MESH
    )


def a2a_kernel(x_ref, o_ref, send, recv):
    m, g = place()
    bar = pltpu.get_barrier_semaphore()
    for d in range(1, 8):
        pl.semaphore_signal(bar, inc=1, device_id=member((m + d) % 8, g), device_id_type=MESH)
    pl.semaphore_wait(bar, 7)
    copies = []
    for d in range(1, 8):
        p = (m + d) % 8
        copies.append(remote(x_ref.at[p], o_ref.at[m], send.at[d], recv.at[d], member(p, g)))
        copies[-1].start()
    o_ref[m] = x_ref[m]
    for copy in copies:
        copy.wait()


def a2a(x, cid):
    return pl.pallas_call(
        a2a_kernel,
        out_shape=jax.ShapeDtypeStruct(x.shape, x.dtype),
        in_specs=[VMEM],
        out_specs=VMEM,
        scratch_shapes=[pltpu.SemaphoreType.DMA((8,)), pltpu.SemaphoreType.DMA((8,))],
        compiler_params=pltpu.CompilerParams(collective_id=cid, has_side_effects=True),
        name="a2a%d" % cid,
    )(x)


def gather_kernel(x_ref, b_ref, m11_ref, m12_ref, m21_ref, s0, r0, s1, r1, s2, r2, s3, r3, s4, r4):
    m, g = place()
    bar = pltpu.get_barrier_semaphore()
    for d in range(1, 8):
        pl.semaphore_signal(bar, inc=1, device_id=member((m + d) % 8, g), device_id_type=MESH)
    for d in range(1, 16):
        pl.semaphore_signal(bar, inc=1, device_id=member(m, (g + d) % 16), device_id_type=MESH)
    pl.semaphore_wait(bar, 22)

    def top(d):
        return remote(x_ref.at[0], m21_ref.at[0, g], s0.at[d], r0.at[g], member(m, (g + d) % 16))

    def part(d):
        p = (g + d) % 16
        return remote(x_ref.at[p], m21_ref.at[p, g], s1.at[d], r1.at[g], member(m, p))

    @pl.when(g < 4)
    def _():
        for d in range(1, 16):
            top(d).start()
        for d in range(1, 16):

            @pl.when((g + d) % 16 != 0)
            def _():
                part(d).start()

        m21_ref[0, g] = x_ref[0]
        m21_ref[g, g] = x_ref[g]

    bands = [
        remote(b_ref, m12_ref.at[m], s2.at[d], r2.at[d], member((m + d) % 8, g))
        for d in range(1, 8)
    ]
    for copy in bands:
        copy.start()
    m12_ref[m] = b_ref[...]
    for s in range(4):

        @pl.when(g != s)
        def _():
            remote(x_ref.at[0], m21_ref.at[0, s], s0.at[0], r0.at[s], member(m, (g + 1) % 16)).wait_recv()

    corners = [
        remote(m21_ref.at[0], m11_ref.at[m], s3.at[d], r3.at[d], member((m + d) % 8, g))
        for d in range(1, 8)
    ]
    for copy in corners:
        copy.start()
    m11_ref[m] = m21_ref[0]

    @pl.when(g != 0)
    def _():
        for s in range(4):

            @pl.when(g != s)
            def _():
                remote(x_ref.at[0], m21_ref.at[g, s], s1.at[0], r1.at[s], member(m, (g + 1) % 16)).wait_recv()

        for d in range(1, 16):
            remote(m21_ref.at[g], m21_ref.at[g], s4.at[d], r4.at[g], member(m, (g + d) % 16)).start()

    for p in range(1, 16):

        @pl.when(g != p)
        def _():
            remote(m21_ref.at[g], m21_ref.at[p], s4.at[0], r4.at[p], member(m, (g + 1) % 16)).wait_recv()

    for copy in corners + bands:
        copy.wait()

    @pl.when(g < 4)
    def _():
        for d in range(1, 16):
            top(d).wait_send()
        for d in range(1, 16):

            @pl.when((g + d) % 16 != 0)
            def _():
                part(d).wait_send()

    @pl.when(g != 0)
    def _():
        for d in range(1, 16):
            remote(m21_ref.at[g], m21_ref.at[g], s4.at[d], r4.at[g], member(m, (g + d) % 16)).wait_send()


def gather(x, b):
    shapes = [(8, 4, 64, 128), (8, 64, 512), (16, 4, 64, 128)]
    counts = [16, 4, 16, 4, 8, 8, 8, 8, 16, 16]
    return pl.pallas_call(
        gather_kernel,
        out_shape=[jax.ShapeDtypeStruct(s, jnp.float32) for s in shapes],
        in_specs=[VMEM] * 2,
        out_specs=[VMEM] * 3,
        scratch_shapes=[pltpu.SemaphoreType.DMA((n,)) for n in counts],
        compiler_params=pltpu.CompilerParams(collective_id=2, has_side_effects=True),
        name="gather",
    )(x, b)


def lu(a):
    n = a.shape[0]
    return pl.pallas_call(
        lu_kernel,
        out_shape=[jax.ShapeDtypeStruct((n, n), jnp.float32)] * 3,
        in_specs=[VMEM],
        out_specs=[VMEM] * 3,
        cost_estimate=pl.CostEstimate(
            flops=40_000_000_000, bytes_accessed=4 << 20, transcendentals=0
        ),
        name="lu",
    )(a)


def spread(x):
    rest = x.shape[1:]
    return jnp.concatenate(
        [x[:512].reshape(8, 64, *rest), x[512:].reshape(8, 192, *rest)], 1
    )


def unspread(x):
    rest = x.shape[2:]
    return jnp.concatenate(
        [x[:, :64].reshape(512, *rest), x[:, 64:].reshape(1536, *rest)], 0
    )


def mixed(x, axis, scale):
    first, second = lax.index_in_dim(x, 0, axis), lax.index_in_dim(x, 1, axis)
    return scale * jnp.concatenate([first + second, first - second], axis) * inv_root


def shards(matrix, row_diag, col_diag):
    m, g = place()
    halves = jnp.stack([spread(matrix[:2048]), spread(matrix[2048:])], 1)
    scales = jnp.stack(
        [jnp.stack([spread(row_diag[l][:2048]), spread(row_diag[l][2048:])], 1) for l in range(2)], 1
    )
    scales = scales.reshape(8, 8, 128)
    across = jnp.broadcast_to(jnp.pad(col_diag, ((0, 6), (0, 0)))[None], (8, 8, 128))
    got = a2a(jnp.concatenate([halves.reshape(8, 512, 128), scales, across], 1), 0)
    body = got[:, :512].reshape(2, 2, 2, 2, 256, 128)
    rd = got[:, 512:520].reshape(2, 4, 2, 2, 256)[:, 0]
    cd = got[:4, 520:522]
    body = mixed(body, 0, rd[:, 0][:, None, None, :, :, None])
    body = mixed(body, 3, rd[:, 1][:, None, None, :, :, None])
    body = mixed(body, 1, cd[:, 0].reshape(1, 2, 2, 1, 1, 128))
    body = mixed(body, 2, cd[:, 1].reshape(1, 2, 2, 1, 1, 128))
    body = body.reshape(2, 4, 512, 128)
    flat = body.transpose(0, 2, 1, 3).reshape(1024, 512)
    corner, band, panel = gather(flat[:, :128].reshape(16, 64, 128), flat[:64])
    corner = corner.transpose(0, 2, 1, 3).reshape(512, 512)
    band = band.reshape(512, 512)
    panel = panel.transpose(0, 2, 1, 3).reshape(1024, 512)
    packed, lower, upper = lu(corner)
    right = hdot(lower, band)
    left = jnp.dot(panel, upper, precision=lax.Precision.HIGH, preferred_element_type=jnp.float32)
    rest = flat - jnp.dot(left, right, precision=lax.Precision.HIGH, preferred_element_type=jnp.float32)
    own = jnp.clip(g, 0, 3) * 128
    first = jnp.where(g < 4, lax.dynamic_slice_in_dim(left, own, 128, 1), rest[:, :128])
    top = lax.dynamic_slice_in_dim(right, 64 * m, 64, 0)
    corner_own = lax.dynamic_slice(packed, (64 * m, own), (64, 128))
    top_first = jnp.where(g < 4, corner_own, top[:, :128])
    done = jnp.concatenate(
        [
            jnp.concatenate([top_first, top[:, 128:]], 1),
            jnp.concatenate([first[64:], rest[64:, 128:]], 1),
        ],
        0,
    )
    back = a2a(done.reshape(2, 512, 4, 128).transpose(0, 2, 1, 3).reshape(8, 512, 128), 1)
    back = back.reshape(8, 2, 256, 128)
    return jnp.concatenate([unspread(back[:, 0]), unspread(back[:, 1])], 0)


def solution(mesh):
    in_specs = (P("row", "col"), P(None, "row"), P(None, "col"))
    out_specs = P("row", "col")
    return jax.shard_map(shards, mesh=mesh, in_specs=in_specs, out_specs=out_specs, check_vma=False)
```

time: 2200 us -> 241 us (0.11)
  the two profiles are of different devices: /device:TPU:6 before, /device:TPU:113 now
where the time goes in v1:
time: 241 us; the launch traced here: 240 us
  Pallas kernels  194 us (80%)
  local copies, waits for them, and re-layouts  26.7 us (11%)
  other arithmetic  11.9 us (5%)
  matrix products  7.1 us (3%)
    pallas_call x2, Pallas kernels, a2a(): pl.pallas_call(a2a_kernel, out_shape=jax.ShapeDtypeStruct(x.shape, x.dtyp...  85.4 us
    pallas_call x1, Pallas kernels, gather(): pl.pallas_call(gather_kernel, out_shape=[jax.ShapeDtypeStruct(s, jnp.floa...  70.4 us
    pallas_call x1, Pallas kernels, lu(): pl.pallas_call(lu_kernel, out_shape=[jax.ShapeDtypeStruct((n, n), jnp.flo...  38.5 us

profile of v1, /device:TPU:113, one launch (start us, length us, event | category | flops | bytes accessed | tf_op | source)
XLA Modules:
  0.0 240.4 jit_solution(8832356533959412336)
XLA Ops:
  2.7 1.5 fusion.8
  4.2 1.1 fusion.7
  6.1 1.5 pad_maximum_fusion.x_ref
  7.6 40.0 %a2a0.1 = f32[8,528,128]{2,1,0:T(8,128)} custom-call(f32[8,528,128]{2,1,0:T(8,128)} %pad_maximum_fusion.x_ref), custom_call_target="tpu_custom_call" | custom-call | tf_op jit(solution)/shard_map/a2a0/pallas_call | solution.py:146
  47.7 1.7 slice_add_fusion.3
  50.5 1.4 copy-done.1
  52.6 1.6 copy.7
  56.4 70.4 %gather.1 = (f32[8,4,64,128]{3,2,1,0:T(8,128)}, f32[8,64,512]{2,1,0:T(8,128)}, f32[16,4,64,128]{3,2,1,0:T(8,128)}) custom-call(f32[16,64,128]{2,1,0:T(8,128)} %bitcast.79, f32[64,512]{1,0:T(8,128)} %slice.212.b_ref), custom_call_target="tpu_custom_call" | custom-call | tf_op jit(solution)/shard_map/gather/pallas_call | solution.py:246
  126.8 1.9 copy.8
  128.7 1.0 copy.23
  129.8 38.5 %lu.1 = (f32[512,512]{1,0:T(8,128)}, f32[512,512]{1,0:T(8,128)}, f32[512,512]{1,0:T(8,128)}) custom-call(f32[512,512]{1,0:T(8,128)} %bitcast.85), custom_call_target="tpu_custom_call" | custom-call | flops 40000000000 | bytes 4194304 | tf_op jit(solution)/shard_map/lu/pallas_call | solution.py:259
  168.2 3.4 %fusion.9 = f32[512,512]{1,0:T(8,128)S(1)} fusion(f32[512,512]{1,0:T(8,128)} %get-tuple-element.13, f32[512,512]{1,0:T(8,128)} %bitcast.81), kind=kOutput, calls=%fused_computation.53 | convolution fusion | flops 1610612736 | bytes 3145728 | tf_op jit(solution)/shard_map/dot_general | solution.py:12
  172.4 3.1 %copy.9 = f32[16,64,4,128]{3,2,1,0:T(4,128)S(1)} copy(f32[16,64,4,128]{3,1,2,0:T(8,128)} %bitcast.80) | data formatting | bytes 4194304 | tf_op jit(solution)/shard_map/transpose | solution.py:311
  175.5 1.9 fusion
  177.4 1.9 convolution_subtract_fusion
  179.3 1.3 copy-done.2
  180.7 1.9 slice_select_fusion
  182.6 2.6 %slice.215 = f32[960,384]{1,0:T(8,128)} slice(f32[1024,512]{1,0:T(8,128)} %copy-done.2), slice={[64:1024], [128:512]} | slice | bytes 2949120 | tf_op jit(solution)/shard_map/slice | solution.py:324
  185.2 1.7 maximum_maximum_fusion
  186.9 1.7 reshape.175
  188.6 3.1 %copy.10 = f32[2,512,4,128]{3,1,2,0:T(8,128)} copy(f32[2,512,4,128]{3,2,1,0:T(4,128)} %reshape.175) | data formatting | bytes 4194304 | tf_op jit(solution)/shard_map/reshape | solution.py:328
  191.7 45.4 %a2a1.1 = f32[8,512,128]{2,1,0:T(8,128)} custom-call(f32[8,512,128]{2,1,0:T(8,128)} %bitcast.69), custom_call_target="tpu_custom_call" | custom-call | tf_op jit(solution)/shard_map/a2a1/pallas_call | solution.py:146
  237.1 1.7 slice_bitcast_fusion.1
  238.9 1.5 pad_maximum_fusion.3
  (57 shorter events, 8.4 us)
Async XLA Ops:
  5.4 0.7 copy-start.4
  47.7 1.7 slice-start
  50.3 1.6 copy-start.1
  172.4 3.1 %copy-start.3 = (f32[512,512]{1,0:T(8,128)S(1)}, f32[512,512]{1,0:T(8,128)}, u32[]{:S(2)}) copy-start(f32[512,512]{1,0:T(8,128)} %get-tuple-element.16) | copy-start | bytes 3145732
  177.4 1.9 copy-start
  179.3 1.3 copy-start.2

commit v2 on v0

v2 whole, which is shorter than its diff:
```python
import jax
import jax.numpy as jnp
from jax import lax
from jax.experimental import pallas as pl
from jax.experimental.pallas import tpu as pltpu
from jax.sharding import PartitionSpec as P

MESH = pl.DeviceIdType.MESH
VMEM = pl.BlockSpec(memory_space=pltpu.VMEM)
GROUP = 4


def split(a):
    high = a.astype(jnp.bfloat16)
    return high, (a - high.astype(jnp.float32)).astype(jnp.bfloat16)


def dot(a, b):
    return jnp.dot(a, b, preferred_element_type=jnp.float32)


def dot3(a, b):
    return dot(a[0], b[0]) + (dot(a[0], b[1]) + dot(a[1], b[0]))


def rows_to(x, height):
    return jnp.broadcast_to(x, (height, x.shape[1]))


def lane_to(x, lane):
    return jnp.broadcast_to(x[:, lane : lane + 1], (x.shape[0], 128))


def lu128(s):
    height = 8 * GROUP
    sub = lax.broadcasted_iota(jnp.int32, (8, 128), 0)
    lane = lax.broadcasted_iota(jnp.int32, (8, 128), 1)
    subs = lax.broadcasted_iota(jnp.int32, (height, 128), 0)
    lanes = lax.broadcasted_iota(jnp.int32, (height, 128), 1)
    count = 16 // GROUP
    tiles = [s[height * t : height * t + height] for t in range(count)]
    extra = [jnp.where(lanes == subs + height * t, 1.0, 0.0) for t in range(count)]
    packed, lower = [], []

    def tall(x):
        return jnp.concatenate([x] * GROUP, 0)

    for b in range(16):
        at, part = b // GROUP, 8 * (b % GROUP)
        rows, rows2 = tiles[at][part : part + 8], extra[at][part : part + 8]
        cols = [lane_to(rows, 8 * b + c) for c in range(8)]
        inv, u = [], {}
        for c in range(8):
            r = 1.0 / rows_to(cols[c][c : c + 1], 8)
            inv.append(tall(r))
            factor = jnp.where(sub > c, cols[c] * r, 0.0)
            top = jnp.where(lane > 8 * b + c, rows_to(rows[c : c + 1], 8), 0.0)
            rows = jnp.where((lane == 8 * b + c) & (sub > c), factor, rows - factor * top)
            if c < 7:
                rows2 = rows2 - factor * rows_to(rows2[c : c + 1], 8)
            for d in range(c + 1, 8):
                row = rows_to(cols[d][c : c + 1], 8)
                u[c, d] = tall(row)
                cols[d] = cols[d] - factor * row
        packed.append(rows)
        lower.append(rows2)
        pieces = [jnp.where(lane == sub + 8 * b, 1.0, 0.0)]
        if part:
            pieces = [tiles[at][:part]] + pieces
        if part + 8 < height:
            pieces = pieces + [tiles[at][part + 8 :]]
        tiles[at] = jnp.concatenate(pieces, 0) if len(pieces) > 1 else pieces[0]
        inside = (lanes >= 8 * b) & (lanes < 8 * b + 8)
        ups, ups2 = [], []
        for c in range(8):
            top = jnp.where(lane >= 8 * b + 8, rows_to(rows[c : c + 1], 8), 0.0)
            ups.append(tall(jnp.where(lane == 8 * b + c, -1.0, top)))
            ups2.append(tall(rows_to(rows2[c : c + 1], 8)))
        for i in range(count):
            t = ((b + 1) // GROUP + i) % count
            tile = tiles[t]
            ls = [lane_to(tile, 8 * b + c) for c in range(8)]
            for c in range(8):
                ls[c] = ls[c] * inv[c]
                for d in range(c + 1, 8):
                    ls[d] = ls[d] - ls[c] * u[c, d]
            tile = jnp.where(inside, 0.0, tile)
            for c in range(8):
                tile = tile - ls[c] * ups[c]
            tiles[t] = tile
            if (t + 1) * GROUP - 1 > b:
                tile = extra[t]
                for c in range(8):
                    tile = tile - ls[c] * ups2[c]
                extra[t] = tile
    return tuple(jnp.concatenate(x, 0) for x in (packed, lower, tiles))


def lu_step(k, packed, li, ui):
    n = ui.shape[0]
    o = pl.multiple_of(k * 128, 128)
    blk = pl.ds(o, 128)
    own, lower, upper = lu128(ui[blk, blk])
    lower, upper = split(lower), split(upper)
    past = lax.broadcasted_iota(jnp.int32, (128, n), 1) >= o + 128
    diag = lax.broadcasted_iota(jnp.int32, (128, n), 1) == (
        lax.broadcasted_iota(jnp.int32, (128, n), 0) + o
    )
    band = ui[blk, :]
    right = dot3(lower, split(band))
    packed[blk, :] = jnp.where(past, right, band)
    packed[blk, blk] = own
    ui[blk, :] = jnp.where(diag, 1.0, 0.0)
    left = dot3(split(ui[:, blk]), upper)
    ui[...] = ui[...] - dot3(split(left), split(jnp.where(past, right, 0.0)))
    ui[:, blk] = left
    lband = dot3(lower, split(li[blk, :]))
    li[blk, :] = lband
    below = lax.broadcasted_iota(jnp.int32, (n, 128), 0) >= o + 128
    li[...] = li[...] - dot3(split(jnp.where(below, left, 0.0)), split(lband))


def kernel(x, s, o, xin, sin, rs, t, m11, m12, m21, packed, li, ui, lh, ll, lf, uf, uh, ul, z, send, recv):
    r, c = lax.axis_index("row"), lax.axis_index("col")
    m, g = r * 4 + c // 16, c % 16
    core, pair = g % 2, g // 2

    def member(p):
        return {"row": p // 4, "col": (p % 4) * 16 + g}

    def chip(d):
        return {"row": r, "col": (m % 4) * 16 + (g + 2 * d) % 16}

    partner = {"row": r, "col": (m % 4) * 16 + g + 1 - 2 * core}

    def device(p):
        return {"row": r, "col": (m % 4) * 16 + p}

    def remote(src, dst, kind, out, into, where):
        return pltpu.make_async_remote_copy(
            src, dst, send.at[kind, out], recv.at[kind, into], device_id=where, device_id_type=MESH
        )

    def rows(p, height, base=0):
        return pl.ds(pl.multiple_of(base + height * p, 8), height)

    def head(d):
        p = (m + d) % 8
        return remote(x.at[:, rows(p, 64)], xin.at[m, :, pl.ds(0, 64)], 0, d, d, member(p))

    def small(d):
        p = (m + d) % 8
        return remote(s.at[p], sin.at[m], 1, d, d, member(p))

    def tail(d, half):
        p = (m + d) % 8
        return remote(
            x.at[half, rows(p, 192, 512)], xin.at[m, half, pl.ds(64, 192)], 2 + half, d, d, member(p)
        )

    def top(d):
        return remote(t.at[0, 0, pl.ds(0, 64)], m21.at[0, core, pair], 4, d, pair, chip(d))

    def top_over():
        return remote(m21.at[0, core], m21.at[0, core], 5, 0, 0, partner)

    def corner(d):
        return remote(m21.at[0, core], m11.at[m, core], 6, d, d, member((m + d) % 8))

    def corner_over(d):
        p = (m + 8 - d) % 8
        return remote(m11.at[p, core], m11.at[p, core], 7, d, d, partner)

    def band(d):
        return remote(t.at[pl.ds(0, 4), 0, pl.ds(0, 64)], m12.at[m], 8, d, d, member((m + d) % 8))

    def piece(p):
        return t.at[(p // 8) * 4, (p % 8) // 4, rows(p % 4, 64)]

    def part(d):
        p = (g + d) % 16
        return remote(piece(p), m21.at[p, core, pair], 9, d, g, device(p))

    def panel(d):
        return remote(m21.at[g], m21.at[g], 10, d, pair, chip(d))

    def panel_over(j):
        p = 2 * j + core
        return remote(m21.at[p], m21.at[p], 11, j, j, partner)

    def back(d, first):
        p = (m + d) % 8
        if first:
            return remote(z.at[p, :, pl.ds(0, 64)], o.at[:, rows(m, 64)], 12, d, d, member(p))
        return remote(z.at[p, :, pl.ds(64, 192)], o.at[:, rows(m, 192, 512)], 13, d, d, member(p))

    bar = pltpu.get_barrier_semaphore()
    for d in range(1, 8):
        pl.semaphore_signal(bar, inc=1, device_id=member((m + d) % 8), device_id_type=MESH)
    for d in range(1, 16):
        pl.semaphore_signal(bar, inc=1, device_id=device((g + d) % 16), device_id_type=MESH)
    pl.semaphore_wait(bar, 22)

    for d in range(1, 8):
        small(d).start()
    for d in range(1, 8):
        head(d).start()
    sin[m] = s[m]
    xin[m, :, 0:64] = x[:, rows(m, 64)]
    xin[m, :, 64:256] = x[:, rows(m, 192, 512)]
    for d in range(1, 8):
        tail(d, 0).start()
    for d in range(1, 8):
        small(d).wait()
    for l in range(2):
        for i in range(2):
            for j in range(2):
                for h in range(2):
                    line = sin[4 * i, 4 * l + 2 * j + h : 4 * l + 2 * j + h + 1, :]
                    rs[l, i, j, 128 * h : 128 * h + 128] = rows_to(line, 128).T

    def mix(j, _):
        at = pl.ds(pl.multiple_of(8 * j, 8), 8)
        first = [rows_to(sin[q, 8:9, :], 8) for q in range(4)]
        second = [rows_to(sin[q, 9:10, :] * 0.25, 8) for q in range(4)]
        for i in range(2):
            mid = {}
            for q in range(4):
                y = []
                for h in range(2):
                    a, b = xin[q, h, at], xin[4 + q, h, at]
                    y.append(rs[0, i, h, at] * (a + b if i == 0 else a - b))
                mid[q] = [rs[1, i, 0, at] * (y[0] + y[1]), rs[1, i, 1, at] * (y[0] - y[1])]
            for h in range(2):
                w = [first[q] * (mid[q][h] + mid[q + 2][h]) for q in range(2)]
                w += [first[q + 2] * (mid[q][h] - mid[q + 2][h]) for q in range(2)]
                for q in (0, 2):
                    t[4 * i + q, h, at] = second[q] * (w[q] + w[q + 1])
                    t[4 * i + q + 1, h, at] = second[q + 1] * (w[q] - w[q + 1])
        return 0

    for d in range(1, 8):
        head(d).wait()
    lax.fori_loop(0, 8, mix, 0)

    @pl.when(g < 4)
    def _():
        for d in range(1, 8):
            top(d).start()
        m21[0, core, pair] = t[0, 0, 0:64]

    for i in range(2):

        @pl.when(g != 2 * i + core)
        def _():
            remote(t.at[0, 0, pl.ds(0, 64)], m21.at[0, core, i], 4, 0, i, partner).wait_recv()

    for d in range(1, 8):
        corner(d).start()
    top_over().start()
    for d in range(1, 8):
        tail(d, 1).start()
    for d in range(1, 8):
        band(d).start()
    m11[m, core] = m21[0, core]
    m12[m] = t[0:4, 0, 0:64]
    li[...] = jnp.where(
        lax.broadcasted_iota(jnp.int32, li.shape, 0) == lax.broadcasted_iota(jnp.int32, li.shape, 1),
        1.0,
        0.0,
    )
    top_over().wait()
    m11[m, 1 - core] = m21[0, 1 - core]
    for d in range(1, 8):
        corner(d).wait_recv()
        corner_over(d).start()
    for d in range(1, 8):
        corner_over(d).wait()
    for i in range(8):
        for j in range(4):
            ui[64 * i : 64 * i + 64, 128 * j : 128 * j + 128] = m11[i, j % 2, j // 2]

    def eliminate(k, _):
        lu_step(k, packed, li, ui)

        @pl.when(k == 0)
        def _():
            for d in range(1, 8):
                tail(d, 0).wait()
                tail(d, 1).wait()
            lax.fori_loop(8, 32, mix, 0)

            @pl.when(g < 4)
            def _():
                for d in range(1, 16):

                    @pl.when((g + d) % 16 != 0)
                    def _():
                        part(d).start()

                @pl.when(g != 0)
                def _():
                    m21[g, core, pair] = t[0, 0, rows(g, 64)]

        @pl.when(k == 1)
        def _():
            @pl.when(g != 0)
            def _():
                for i in range(4):

                    @pl.when(g != i)
                    def _():
                        remote(
                            piece(g), m21.at[g, i % 2, i // 2], 9, 0, i, partner
                        ).wait_recv()

                for d in range(1, 8):
                    panel(d).start()
                panel_over(pair).start()

        @pl.when(k == 2)
        def _():
            for j in range(8):

                @pl.when((2 * j + core != 0) & (j != pair))
                def _():
                    remote(m21.at[g], m21.at[2 * j + core], 10, 0, j, partner).wait_recv()
                    panel_over(j).start()

        return 0

    lax.fori_loop(0, 4, eliminate, 0)

    for d in range(1, 8):
        corner(d).wait_send()
        band(d).wait()
    lower = split(li[...])
    for q in range(4):
        lanes = slice(128 * q, 128 * q + 128)
        uf[:, lanes] = dot3(lower, split(m12[:, q].reshape(512, 128)))
        uh[:, lanes], ul[:, lanes] = split(uf[:, lanes])

    @pl.when(g < 4)
    def _():
        for d in range(1, 8):
            top(d).wait_send()
        for d in range(1, 16):

            @pl.when((g + d) % 16 != 0)
            def _():
                part(d).wait_send()

    @pl.when(g != 0)
    def _():
        for d in range(1, 8):
            panel(d).wait_send()

    for j in range(8):

        @pl.when(2 * j + core != 0)
        def _():
            panel_over(j).wait_send()

        @pl.when(2 * j + 1 - core != 0)
        def _():
            remote(m21.at[g], m21.at[2 * j + 1 - core], 11, 0, j, partner).wait_recv()

    upper = split(ui[...])
    for i in range(2):
        cols = [m21[8 * i : 8 * i + 8, j % 2, j // 2].reshape(512, 128) for j in range(4)]
        got = dot3(split(jnp.concatenate(cols, 1)), upper)
        lf[i] = got
        lh[i], ll[i] = split(got)

    own = pl.ds(pl.multiple_of(jnp.minimum(g, 3) * 128, 128), 128)

    def finish(d, _):
        p = (m + d) % 8
        i, q = p // 4, p % 4
        lanes = pl.ds(pl.multiple_of(128 * q, 128), 128)
        got = dot3((lh[i], ll[i]), (uh[:, lanes], ul[:, lanes]))
        z[p] = t[p] - got.reshape(2, 256, 128)

        @pl.when((q == 0) & (g < 4))
        def _():
            z[p] = lf[i, :, own].reshape(2, 256, 128)

        @pl.when(i == 0)
        def _():
            z[p, 0, 0:64] = uf[rows(m, 64), lanes]

        @pl.when((p == 0) & (g < 4))
        def _():
            z[p, 0, 0:64] = packed[rows(m, 64), own]

        @pl.when(d < 8)
        def _():
            back(d, True).start()
            back(d, False).start()

        return 0

    lax.fori_loop(1, 9, finish, 0)
    o[:, rows(m, 64)] = z[m, :, 0:64]
    o[:, rows(m, 192, 512)] = z[m, :, 64:256]
    for d in range(1, 8):
        back(d, True).wait()
        back(d, False).wait()


def spread(x):
    return jnp.concatenate([x[:512].reshape(8, 64), x[512:].reshape(8, 192)], 1)


def shards(matrix, row_diag, col_diag):
    scales = [spread(row_diag[l, 2048 * h : 2048 * h + 2048]) for l in range(2) for h in range(2)]
    scales = jnp.stack(scales, 1).reshape(8, 8, 128)
    across = jnp.broadcast_to(jnp.pad(col_diag, ((0, 6), (0, 0)))[None], (8, 8, 128))
    f32, bf16 = jnp.float32, jnp.bfloat16
    shapes = [
        ((8, 2, 256, 128), f32),
        ((8, 16, 128), f32),
        ((2, 2, 2, 256, 128), f32),
        ((8, 2, 256, 128), f32),
        ((8, 2, 2, 64, 128), f32),
        ((8, 4, 64, 128), f32),
        ((16, 2, 2, 64, 128), f32),
        ((512, 512), f32),
        ((512, 512), f32),
        ((512, 512), f32),
        ((2, 512, 512), bf16),
        ((2, 512, 512), bf16),
        ((2, 512, 512), f32),
        ((512, 512), f32),
        ((512, 512), bf16),
        ((512, 512), bf16),
        ((8, 2, 256, 128), f32),
    ]
    out = pl.pallas_call(
        kernel,
        out_shape=jax.ShapeDtypeStruct((2, 2048, 128), f32),
        in_specs=[VMEM] * 2,
        out_specs=VMEM,
        scratch_shapes=[pltpu.VMEM(*shape) for shape in shapes]
        + [pltpu.SemaphoreType.DMA((14, 16))] * 2,
        compiler_params=pltpu.CompilerParams(collective_id=0, has_side_effects=True),
        name="whole",
    )(matrix.reshape(2, 2048, 128), jnp.concatenate([scales, across], 1))
    return out.reshape(4096, 128)


def solution(mesh):
    in_specs = (P("row", "col"), P(None, "row"), P(None, "col"))
    out_specs = P("row", "col")
    return jax.shard_map(shards, mesh=mesh, in_specs=in_specs, out_specs=out_specs, check_vma=False)
```

time: 2200 us -> 132 us (0.06)
  the two profiles are of different devices: /device:TPU:6 before, /device:TPU:84 now
where the time goes in v2:
time: 132 us
  Pallas kernels  125 us (95%)
  local copies, waits for them, and re-layouts  6.02 us (5%)
    pallas_call x1, Pallas kernels, shards(): pl.pallas_call(kernel, out_shape=jax.ShapeDtypeStruct((2, 2048, 128), f32...  125 us
    unnamed x1, local copies, waits for them, and re-layouts  3.05 us

profile of v2, /device:TPU:84, one launch (start us, length us, event | category | flops | bytes accessed | tf_op | source)
XLA Modules:
  0.0 131.7 jit_solution(1180965622043846358)
XLA Ops:
  0.0 0.7 pad.4
  0.7 0.8 slice_reduce_fusion.7
  1.5 0.1 reshape.51
  1.6 0.1 reshape.55
  1.6 0.1 reshape.53
  1.7 0.1 reshape.57
  1.8 0.9 slice_reduce_fusion.3
  2.6 0.1 reshape.52
  2.7 0.1 pad_maximum_fusion.2
  2.8 0.1 reshape.56
  2.9 0.1 pad_maximum_fusion.4
  3.0 0.1 reshape.54
  3.0 0.1 pad_maximum_fusion.3
  3.1 0.1 reshape.58
  3.2 0.1 pad_maximum_fusion.5
  3.3 0.6 pad_maximum_fusion.s
  4.0 124.7 %whole.1 = f32[2,2048,128]{2,1,0:T(8,128)} custom-call(f32[2,2048,128]{2,1,0:T(8,128)} %bitcast.3, f32[8,16,128]{2,1,0:T(8,128)} %pad_maximum_fusion.s), custom_call_target="tpu_custom_call" | custom-call | tf_op jit(solution)/shard_map/whole/pallas_call | solution.py:439
  128.7 3.0 %copy.5 = f32[4096,128]{1,0:T(8,128)} copy(f32[4096,128]{1,0:T(8,128)} %bitcast.2) | data formatting | bytes 4194304
  (7 shorter events, 0.1 us)

commit v3 on v2

--- a/solution.py
+++ b/solution.py
@@ -1,3 +1,5 @@
+import functools
+
 import jax
 import jax.numpy as jnp
 from jax import lax
@@ -8,6 +10,7 @@
 MESH = pl.DeviceIdType.MESH
 VMEM = pl.BlockSpec(memory_space=pltpu.VMEM)
 GROUP = 4
+EARLY = (1, 2, 4, 6)
 
 
 def split(a):
@@ -120,9 +123,10 @@
     li[...] = li[...] - dot3(split(jnp.where(below, left, 0.0)), split(lband))
 
 
-def kernel(x, s, o, xin, sin, rs, t, m11, m12, m21, packed, li, ui, lh, ll, lf, uf, uh, ul, z, send, recv):
+def kernel(hbm, rd, cd, o, x, rdo, cds, xin, rs, t, m11, m12, m21, packed, li, ui, lh, ll, lf, uf, uh, ul, z, send, recv, load):
     r, c = lax.axis_index("row"), lax.axis_index("col")
-    m, g = r * 4 + c // 16, c % 16
+    q, g = c // 16, c % 16
+    m = r * 4 + q
     core, pair = g % 2, g // 2
 
     def member(p):
@@ -149,8 +153,9 @@
         return remote(x.at[:, rows(p, 64)], xin.at[m, :, pl.ds(0, 64)], 0, d, d, member(p))
 
     def small(d):
-        p = (m + d) % 8
-        return remote(s.at[p], sin.at[m], 1, d, d, member(p))
+        if d == 0:
+            return remote(rd, rdo, 1, 0, 0, member((m + 4) % 8))
+        return remote(cd, cds.at[q], 1, d, d, member(r * 4 + (q + d) % 4))
 
     def tail(d, half):
         p = (m + d) % 8
@@ -188,11 +193,22 @@
         p = 2 * j + core
         return remote(m21.at[p], m21.at[p], 11, j, j, partner)
 
-    def back(d, first):
-        p = (m + d) % 8
+    def target(slot):
+        half = slot // 4
+        return 4 * ((r + 1 + half) % 2) + (q + slot + half) % 4
+
+    def back(slot, first):
+        p = target(slot)
         if first:
-            return remote(z.at[p, :, pl.ds(0, 64)], o.at[:, rows(m, 64)], 12, d, d, member(p))
-        return remote(z.at[p, :, pl.ds(64, 192)], o.at[:, rows(m, 192, 512)], 13, d, d, member(p))
+            return remote(z.at[p, :, pl.ds(0, 64)], o.at[:, rows(m, 64)], 12, slot, slot, member(p))
+        return remote(z.at[p, :, pl.ds(64, 192)], o.at[:, rows(m, 192, 512)], 13, slot, slot, member(p))
+
+    loads = [
+        pltpu.make_async_copy(hbm.at[:, pl.ds(0, 512)], x.at[:, pl.ds(0, 512)], load.at[0]),
+        pltpu.make_async_copy(hbm.at[:, pl.ds(512, 1536)], x.at[:, pl.ds(512, 1536)], load.at[1]),
+    ]
+    for copy in loads:
+        copy.start()
 
     bar = pltpu.get_barrier_semaphore()
     for d in range(1, 8):
@@ -201,36 +217,44 @@
         pl.semaphore_signal(bar, inc=1, device_id=device((g + d) % 16), device_id_type=MESH)
     pl.semaphore_wait(bar, 22)
 
-    for d in range(1, 8):
+    for d in range(4):
         small(d).start()
+    loads[0].wait()
     for d in range(1, 8):
         head(d).start()
-    sin[m] = s[m]
+    cds[q] = cd[...]
     xin[m, :, 0:64] = x[:, rows(m, 64)]
+    loads[1].wait()
+    for d in EARLY:
+        tail(d, 0).start()
     xin[m, :, 64:256] = x[:, rows(m, 192, 512)]
-    for d in range(1, 8):
-        tail(d, 0).start()
-    for d in range(1, 8):
+
+    def widen(source, i):
+        for l in range(2):
+            for h in range(2):
+                for j in range(3):
+                    at = 16 * h + (m // 2 if j == 0 else 3 + j + 3 * m // 2)
+                    line = source[l : l + 1, pl.ds(pl.multiple_of(128 * at, 128), 128)]
+                    rs[l, i, h, 128 * j : 128 * j + 128] = rows_to(line, 128).T
+
+    widen(rd, r)
+    for d in range(4):
         small(d).wait()
-    for l in range(2):
-        for i in range(2):
-            for j in range(2):
-                for h in range(2):
-                    line = sin[4 * i, 4 * l + 2 * j + h : 4 * l + 2 * j + h + 1, :]
-                    rs[l, i, j, 128 * h : 128 * h + 128] = rows_to(line, 128).T
-
-    def mix(j, _):
+    widen(rdo, 1 - r)
+
+    def mix(base, j, _):
         at = pl.ds(pl.multiple_of(8 * j, 8), 8)
-        first = [rows_to(sin[q, 8:9, :], 8) for q in range(4)]
-        second = [rows_to(sin[q, 9:10, :] * 0.25, 8) for q in range(4)]
+        to = pl.ds(pl.multiple_of(8 * j + base + 64 * (m % 2), 8), 8)
+        first = [rows_to(cds[q, 0:1, :], 8) for q in range(4)]
+        second = [rows_to(cds[q, 1:2, :] * 0.25, 8) for q in range(4)]
         for i in range(2):
             mid = {}
             for q in range(4):
                 y = []
                 for h in range(2):
                     a, b = xin[q, h, at], xin[4 + q, h, at]
-                    y.append(rs[0, i, h, at] * (a + b if i == 0 else a - b))
-                mid[q] = [rs[1, i, 0, at] * (y[0] + y[1]), rs[1, i, 1, at] * (y[0] - y[1])]
+                    y.append(rs[0, i, h, to] * (a + b if i == 0 else a - b))
+                mid[q] = [rs[1, i, 0, to] * (y[0] + y[1]), rs[1, i, 1, to] * (y[0] - y[1])]
             for h in range(2):
                 w = [first[q] * (mid[q][h] + mid[q + 2][h]) for q in range(2)]
                 w += [first[q + 2] * (mid[q][h] - mid[q + 2][h]) for q in range(2)]
@@ -241,7 +265,7 @@
 
     for d in range(1, 8):
         head(d).wait()
-    lax.fori_loop(0, 8, mix, 0)
+    lax.fori_loop(0, 8, functools.partial(mix, 0), 0)
 
     @pl.when(g < 4)
     def _():
@@ -259,6 +283,8 @@
         corner(d).start()
     top_over().start()
     for d in range(1, 8):
+        if d not in EARLY:
+            tail(d, 0).start()
         tail(d, 1).start()
     for d in range(1, 8):
         band(d).start()
@@ -288,7 +314,7 @@
             for d in range(1, 8):
                 tail(d, 0).wait()
                 tail(d, 1).wait()
-            lax.fori_loop(8, 32, mix, 0)
+            lax.fori_loop(8, 32, functools.partial(mix, 64), 0)
 
             @pl.when(g < 4)
             def _():
@@ -318,27 +344,79 @@
                     panel(d).start()
                 panel_over(pair).start()
 
-        @pl.when(k == 2)
-        def _():
-            for j in range(8):
-
-                @pl.when((2 * j + core != 0) & (j != pair))
-                def _():
-                    remote(m21.at[g], m21.at[2 * j + core], 10, 0, j, partner).wait_recv()
-                    panel_over(j).start()
-
         return 0
 
     lax.fori_loop(0, 4, eliminate, 0)
 
-    for d in range(1, 8):
-        corner(d).wait_send()
+    def relay(i):
+        for k in range(4):
+            j = 4 * i + k
+
+            @pl.when((2 * j + core != 0) & (j != pair))
+            def _():
+                remote(m21.at[g], m21.at[2 * j + core], 10, 0, j, partner).wait_recv()
+                panel_over(j).start()
+
+    def left_of(i):
+        for k in range(4):
+            j = 4 * i + k
+
+            @pl.when(2 * j + 1 - core != 0)
+            def _():
+                remote(m21.at[g], m21.at[2 * j + 1 - core], 11, 0, j, partner).wait_recv()
+
+        at = pl.ds(8 * i, 8)
+        cols = [m21[at, j % 2, j // 2].reshape(512, 128) for j in range(4)]
+        got = dot3(split(jnp.concatenate(cols, 1)), split(ui[...]))
+        lf[i] = got
+        lh[i], ll[i] = split(got)
+
+    own = pl.ds(pl.multiple_of(jnp.minimum(g, 3) * 128, 128), 128)
+
+    def finish(slot, _):
+        p = target(slot)
+        i = p // 4
+        lanes = pl.ds(pl.multiple_of(128 * (p % 4), 128), 128)
+        got = dot3((lh[i], ll[i]), (uh[:, lanes], ul[:, lanes]))
+        z[p] = t[p] - got.reshape(2, 256, 128)
+
+        @pl.when((p % 4 == 0) & (g < 4))
+        def _():
+            z[p] = lf[i, :, own].reshape(2, 256, 128)
+
+        @pl.when(i == 0)
+        def _():
+            z[p, 0, 0:64] = uf[rows(m, 64), lanes]
+
+        @pl.when((p == 0) & (g < 4))
+        def _():
+            z[p, 0, 0:64] = packed[rows(m, 64), own]
+
+        @pl.when(slot < 7)
+        def _():
+            back(slot, True).start()
+            back(slot, False).start()
+
+        return 0
+
+    relay(1 - r)
+    for d in range(1, 8):
         band(d).wait()
     lower = split(li[...])
-    for q in range(4):
-        lanes = slice(128 * q, 128 * q + 128)
-        uf[:, lanes] = dot3(lower, split(m12[:, q].reshape(512, 128)))
+    for j in range(4):
+        lanes = slice(128 * j, 128 * j + 128)
+        uf[:, lanes] = dot3(lower, split(m12[:, j].reshape(512, 128)))
         uh[:, lanes], ul[:, lanes] = split(uf[:, lanes])
+    left_of(1 - r)
+    relay(r)
+    lax.fori_loop(0, 4, finish, 0)
+    left_of(r)
+    lax.fori_loop(4, 8, finish, 0)
+    o[:, rows(m, 64)] = z[m, :, 0:64]
+    o[:, rows(m, 192, 512)] = z[m, :, 64:256]
+
+    for d in range(1, 8):
+        corner(d).wait_send()
 
     @pl.when(g < 4)
     def _():
@@ -361,66 +439,19 @@
         def _():
             panel_over(j).wait_send()
 
-        @pl.when(2 * j + 1 - core != 0)
-        def _():
-            remote(m21.at[g], m21.at[2 * j + 1 - core], 11, 0, j, partner).wait_recv()
-
-    upper = split(ui[...])
-    for i in range(2):
-        cols = [m21[8 * i : 8 * i + 8, j % 2, j // 2].reshape(512, 128) for j in range(4)]
-        got = dot3(split(jnp.concatenate(cols, 1)), upper)
-        lf[i] = got
-        lh[i], ll[i] = split(got)
-
-    own = pl.ds(pl.multiple_of(jnp.minimum(g, 3) * 128, 128), 128)
-
-    def finish(d, _):
-        p = (m + d) % 8
-        i, q = p // 4, p % 4
-        lanes = pl.ds(pl.multiple_of(128 * q, 128), 128)
-        got = dot3((lh[i], ll[i]), (uh[:, lanes], ul[:, lanes]))
-        z[p] = t[p] - got.reshape(2, 256, 128)
-
-        @pl.when((q == 0) & (g < 4))
-        def _():
-            z[p] = lf[i, :, own].reshape(2, 256, 128)
-
-        @pl.when(i == 0)
-        def _():
-            z[p, 0, 0:64] = uf[rows(m, 64), lanes]
-
-        @pl.when((p == 0) & (g < 4))
-        def _():
-            z[p, 0, 0:64] = packed[rows(m, 64), own]
-
-        @pl.when(d < 8)
-        def _():
-            back(d, True).start()
-            back(d, False).start()
-
-        return 0
-
-    lax.fori_loop(1, 9, finish, 0)
-    o[:, rows(m, 64)] = z[m, :, 0:64]
-    o[:, rows(m, 192, 512)] = z[m, :, 64:256]
-    for d in range(1, 8):
-        back(d, True).wait()
-        back(d, False).wait()
-
-
-def spread(x):
-    return jnp.concatenate([x[:512].reshape(8, 64), x[512:].reshape(8, 192)], 1)
+    for slot in range(7):
+        back(slot, True).wait()
+        back(slot, False).wait()
 
 
 def shards(matrix, row_diag, col_diag):
-    scales = [spread(row_diag[l, 2048 * h : 2048 * h + 2048]) for l in range(2) for h in range(2)]
-    scales = jnp.stack(scales, 1).reshape(8, 8, 128)
-    across = jnp.broadcast_to(jnp.pad(col_diag, ((0, 6), (0, 0)))[None], (8, 8, 128))
     f32, bf16 = jnp.float32, jnp.bfloat16
     shapes = [
+        ((2, 2048, 128), f32),
+        ((2, 4096), f32),
+        ((4, 2, 128), f32),
         ((8, 2, 256, 128), f32),
-        ((8, 16, 128), f32),
-        ((2, 2, 2, 256, 128), f32),
+        ((2, 2, 2, 384, 128), f32),
         ((8, 2, 256, 128), f32),
         ((8, 2, 2, 64, 128), f32),
         ((8, 4, 64, 128), f32),
@@ -438,14 +469,15 @@
     ]
     out = pl.pallas_call(
         kernel,
-        out_shape=jax.ShapeDtypeStruct((2, 2048, 128), f32),
-        in_specs=[VMEM] * 2,
+        out_shape=pltpu.VMEM((2, 2048, 128), f32),
+        in_specs=[pl.BlockSpec(memory_space=pl.ANY), VMEM, VMEM],
         out_specs=VMEM,
         scratch_shapes=[pltpu.VMEM(*shape) for shape in shapes]
-        + [pltpu.SemaphoreType.DMA((14, 16))] * 2,
+        + [pltpu.SemaphoreType.DMA((14, 16))] * 2
+        + [pltpu.SemaphoreType.DMA((2,))],
         compiler_params=pltpu.CompilerParams(collective_id=0, has_side_effects=True),
         name="whole",
-    )(matrix.reshape(2, 2048, 128), jnp.concatenate([scales, across], 1))
+    )(matrix.reshape(2, 2048, 128), row_diag, col_diag)
     return out.reshape(4096, 128)
 
 

time: 132 us -> 113 us (0.86)
  the two profiles are of different devices: /device:TPU:84 before, /device:TPU:6 now
where the time goes in v3:
time: 113 us; the launch traced here: 111 us
  Pallas kernels  109 us (96%)
  local copies, waits for them, and re-layouts  1.32 us (1%)
    pallas_call x1, Pallas kernels, shards(): pl.pallas_call(kernel, out_shape=pltpu.VMEM((2, 2048, 128), f32), in_spec...  109 us

profile of v3, /device:TPU:6, one launch (start us, length us, event | category | flops | bytes accessed | tf_op | source)
XLA Modules:
  0.0 110.8 jit_solution(10600052216823237772)
XLA Ops:
  0.0 109.4 %whole.1 = f32[2,2048,128]{2,1,0:T(8,128)S(1)} custom-call(f32[2,2048,128]{2,1,0:T(8,128)} %bitcast.3, f32[2,4096]{1,0:T(2,128)} %rd.1, f32[2,128]{1,0:T(2,128)} %cd.1), custom_call_target="tpu_custom_call" | custom-call | tf_op jit(solution)/shard_map/whole/pallas_call | solution.py:470
  109.4 1.3 %copy.5 = f32[4096,128]{1,0:T(8,128)} copy(f32[4096,128]{1,0:T(8,128)S(1)} %bitcast.2) | data formatting | bytes 4194304

commit v4 on v3

--- a/solution.py
+++ b/solution.py
@@ -52,19 +52,24 @@
         at, part = b // GROUP, 8 * (b % GROUP)
         rows, rows2 = tiles[at][part : part + 8], extra[at][part : part + 8]
         cols = [lane_to(rows, 8 * b + c) for c in range(8)]
-        inv, u = [], {}
+        inner = (lane >= 8 * b) & (lane < 8 * b + 8)
+        full = jnp.where(lane >= 8 * b + 8, rows, jnp.where(lane == sub + 8 * b, -1.0, 0.0))
+        full2 = rows2
         for c in range(8):
-            r = 1.0 / rows_to(cols[c][c : c + 1], 8)
-            inv.append(tall(r))
-            factor = jnp.where(sub > c, cols[c] * r, 0.0)
+            column = cols[c]
+            r = 1.0 / rows_to(column[c : c + 1], 8)
+            factor = jnp.where(sub > c, column * r, 0.0)
+            for d in range(c + 1, 8):
+                row = rows_to(cols[d][c : c + 1], 8) * r
+                cols[d] = jnp.where(sub == c, row, cols[d] - column * row)
+            row = rows_to(full[c : c + 1], 8) * r
+            full = jnp.where(sub == c, row, full - jnp.where(inner & (sub > c), 0.0, column) * row)
+            row = rows_to(full2[c : c + 1], 8) * r
+            full2 = jnp.where(sub == c, row, full2 - column * row)
             top = jnp.where(lane > 8 * b + c, rows_to(rows[c : c + 1], 8), 0.0)
             rows = jnp.where((lane == 8 * b + c) & (sub > c), factor, rows - factor * top)
             if c < 7:
                 rows2 = rows2 - factor * rows_to(rows2[c : c + 1], 8)
-            for d in range(c + 1, 8):
-                row = rows_to(cols[d][c : c + 1], 8)
-                u[c, d] = tall(row)
-                cols[d] = cols[d] - factor * row
         packed.append(rows)
         lower.append(rows2)
         pieces = [jnp.where(lane == sub + 8 * b, 1.0, 0.0)]
@@ -74,19 +79,12 @@
             pieces = pieces + [tiles[at][part + 8 :]]
         tiles[at] = jnp.concatenate(pieces, 0) if len(pieces) > 1 else pieces[0]
         inside = (lanes >= 8 * b) & (lanes < 8 * b + 8)
-        ups, ups2 = [], []
-        for c in range(8):
-            top = jnp.where(lane >= 8 * b + 8, rows_to(rows[c : c + 1], 8), 0.0)
-            ups.append(tall(jnp.where(lane == 8 * b + c, -1.0, top)))
-            ups2.append(tall(rows_to(rows2[c : c + 1], 8)))
+        ups = [tall(rows_to(full[c : c + 1], 8)) for c in range(8)]
+        ups2 = [tall(rows_to(full2[c : c + 1], 8)) for c in range(8)]
         for i in range(count):
             t = ((b + 1) // GROUP + i) % count
             tile = tiles[t]
             ls = [lane_to(tile, 8 * b + c) for c in range(8)]
-            for c in range(8):
-                ls[c] = ls[c] * inv[c]
-                for d in range(c + 1, 8):
-                    ls[d] = ls[d] - ls[c] * u[c, d]
             tile = jnp.where(inside, 0.0, tile)
             for c in range(8):
                 tile = tile - ls[c] * ups[c]
@@ -123,7 +121,7 @@
     li[...] = li[...] - dot3(split(jnp.where(below, left, 0.0)), split(lband))
 
 
-def kernel(hbm, rd, cd, o, x, rdo, cds, xin, rs, t, m11, m12, m21, packed, li, ui, lh, ll, lf, uf, uh, ul, z, send, recv, load):
+def kernel(hbm, rd, cd, o, x, rdo, cds, xin, rs, t, m11, m12, m21, packed, li, ui, mh, ml, uf, wh, wl, lih, lil, uih, uil, z, send, recv, load):
     r, c = lax.axis_index("row"), lax.axis_index("col")
     q, g = c // 16, c % 16
     m = r * 4 + q
@@ -157,10 +155,15 @@
             return remote(rd, rdo, 1, 0, 0, member((m + 4) % 8))
         return remote(cd, cds.at[q], 1, d, d, member(r * 4 + (q + d) % 4))
 
-    def tail(d, half):
+    def tail(d, unit):
         p = (m + d) % 8
         return remote(
-            x.at[half, rows(p, 192, 512)], xin.at[m, half, pl.ds(64, 192)], 2 + half, d, d, member(p)
+            x.at[:, pl.ds(pl.multiple_of(192 * p + 448 + 64 * unit, 8), 64)],
+            xin.at[m, :, pl.ds(64 * unit, 64)],
+            (0, 2, 3, 14)[unit],
+            d,
+            d,
+            member(p),
         )
 
     def top(d):
@@ -182,12 +185,66 @@
     def piece(p):
         return t.at[(p // 8) * 4, (p % 8) // 4, rows(p % 4, 64)]
 
-    def part(d):
-        p = (g + d) % 16
-        return remote(piece(p), m21.at[p, core, pair], 9, d, g, device(p))
-
-    def panel(d):
-        return remote(m21.at[g], m21.at[g], 10, d, pair, chip(d))
+    def part(p, plane):
+        return pltpu.make_async_remote_copy(
+            piece(p),
+            m21.at[p, core, pair],
+            send.at[9 + 6 * plane, p],
+            recv.at[9, g + 4 * (p // 8)],
+            device_id=device(8 * plane + p % 8),
+            device_id_type=MESH,
+        )
+
+    def parts(unit):
+        @pl.when(g < 4)
+        def _():
+            for i in range(4):
+                p = 4 * i + unit
+                if p == 0:
+                    continue
+                part(p, 1).start()
+                if p % 8 >= 4:
+                    part(p, 0).start()
+                else:
+
+                    @pl.when(g != p % 8)
+                    def _():
+                        part(p, 0).start()
+
+                    @pl.when(g == p % 8)
+                    def _():
+                        m21[p, core, pair] = piece(p)[...]
+
+    def spread(unit):
+        @pl.when(g % 4 == unit)
+        def _():
+            for e in range(2):
+
+                @pl.when(here + 8 * e != 0)
+                def _():
+                    for i in range(4):
+
+                        @pl.when(g != i)
+                        def _():
+                            remote(
+                                piece(here), m21.at[here + 8 * e, i % 2, i // 2], 9, 0, i + 4 * e, partner
+                            ).wait_recv()
+
+                    for d in range(1, 4):
+                        panel(e, d).start()
+                    panel_over(here // 2 + 4 * e).start()
+
+    def arrive(unit):
+        for d in range(1, 8):
+            tail(d, unit).wait()
+        lax.fori_loop(8 * unit, 8 * unit + 8, functools.partial(mix, 64), 0)
+
+    here = g % 8
+
+    def panel(e, d):
+        p = here + 8 * e
+        where = device(8 * (g // 8) + (here + 2 * d) % 8)
+        return remote(m21.at[p], m21.at[p], 10, 4 * e + d, here // 2 + 4 * e, where)
 
     def panel_over(j):
         p = 2 * j + core
@@ -226,7 +283,7 @@
     xin[m, :, 0:64] = x[:, rows(m, 64)]
     loads[1].wait()
     for d in EARLY:
-        tail(d, 0).start()
+        tail(d, 1).start()
     xin[m, :, 64:256] = x[:, rows(m, 192, 512)]
 
     def widen(source, i):
@@ -273,6 +330,8 @@
             top(d).start()
         m21[0, core, pair] = t[0, 0, 0:64]
 
+    parts(0)
+
     for i in range(2):
 
         @pl.when(g != 2 * i + core)
@@ -284,10 +343,10 @@
     top_over().start()
     for d in range(1, 8):
         if d not in EARLY:
-            tail(d, 0).start()
-        tail(d, 1).start()
-    for d in range(1, 8):
-        band(d).start()
+            tail(d, 1).start()
+    for unit in (2, 3):
+        for d in range(1, 8):
+            tail(d, unit).start()
     m11[m, core] = m21[0, core]
     m12[m] = t[0:4, 0, 0:64]
     li[...] = jnp.where(
@@ -306,43 +365,30 @@
         for j in range(4):
             ui[64 * i : 64 * i + 64, 128 * j : 128 * j + 128] = m11[i, j % 2, j // 2]
 
+    spread(0)
+
     def eliminate(k, _):
         lu_step(k, packed, li, ui)
 
         @pl.when(k == 0)
         def _():
+            arrive(1)
+            parts(1)
+            arrive(2)
+            parts(2)
             for d in range(1, 8):
-                tail(d, 0).wait()
-                tail(d, 1).wait()
-            lax.fori_loop(8, 32, functools.partial(mix, 64), 0)
-
-            @pl.when(g < 4)
-            def _():
-                for d in range(1, 16):
-
-                    @pl.when((g + d) % 16 != 0)
-                    def _():
-                        part(d).start()
-
-                @pl.when(g != 0)
-                def _():
-                    m21[g, core, pair] = t[0, 0, rows(g, 64)]
+                band(d).start()
 
         @pl.when(k == 1)
         def _():
-            @pl.when(g != 0)
-            def _():
-                for i in range(4):
-
-                    @pl.when(g != i)
-                    def _():
-                        remote(
-                            piece(g), m21.at[g, i % 2, i // 2], 9, 0, i, partner
-                        ).wait_recv()
-
-                for d in range(1, 8):
-                    panel(d).start()
-                panel_over(pair).start()
+            arrive(3)
+            parts(3)
+            spread(1)
+            spread(2)
+
+        @pl.when(k == 2)
+        def _():
+            spread(3)
 
         return 0
 
@@ -352,9 +398,9 @@
         for k in range(4):
             j = 4 * i + k
 
-            @pl.when((2 * j + core != 0) & (j != pair))
+            @pl.when((2 * j + core != 0) & (j != here // 2 + 4 * i))
             def _():
-                remote(m21.at[g], m21.at[2 * j + core], 10, 0, j, partner).wait_recv()
+                remote(m21.at[here], m21.at[2 * j + core], 10, 0, j, partner).wait_recv()
                 panel_over(j).start()
 
     def left_of(i):
@@ -363,26 +409,32 @@
 
             @pl.when(2 * j + 1 - core != 0)
             def _():
-                remote(m21.at[g], m21.at[2 * j + 1 - core], 11, 0, j, partner).wait_recv()
+                remote(m21.at[here], m21.at[2 * j + 1 - core], 11, 0, j, partner).wait_recv()
 
         at = pl.ds(8 * i, 8)
-        cols = [m21[at, j % 2, j // 2].reshape(512, 128) for j in range(4)]
-        got = dot3(split(jnp.concatenate(cols, 1)), split(ui[...]))
-        lf[i] = got
-        lh[i], ll[i] = split(got)
+        for j in range(4):
+            lanes = slice(128 * j, 128 * j + 128)
+            mh[i, :, lanes], ml[i, :, lanes] = split(m21[at, j % 2, j // 2].reshape(512, 128))
 
     own = pl.ds(pl.multiple_of(jnp.minimum(g, 3) * 128, 128), 128)
+
+    def prepare(slot):
+        j = (q + slot) % 4
+        lanes = pl.ds(pl.multiple_of(128 * j, 128), 128)
+        right = dot3((lih[...], lil[...]), split(m12[:, j].reshape(512, 128)))
+        uf[:, lanes] = right
+        wh[:, lanes], wl[:, lanes] = split(dot3((uih[...], uil[...]), split(right)))
 
     def finish(slot, _):
         p = target(slot)
         i = p // 4
         lanes = pl.ds(pl.multiple_of(128 * (p % 4), 128), 128)
-        got = dot3((lh[i], ll[i]), (uh[:, lanes], ul[:, lanes]))
+        got = dot3((mh[i], ml[i]), (wh[:, lanes], wl[:, lanes]))
         z[p] = t[p] - got.reshape(2, 256, 128)
 
         @pl.when((p % 4 == 0) & (g < 4))
         def _():
-            z[p] = lf[i, :, own].reshape(2, 256, 128)
+            z[p] = dot3((mh[i], ml[i]), (uih[:, own], uil[:, own])).reshape(2, 256, 128)
 
         @pl.when(i == 0)
         def _():
@@ -397,16 +449,18 @@
             back(slot, True).start()
             back(slot, False).start()
 
+        @pl.when(slot < 3)
+        def _():
+            prepare(slot + 1)
+
         return 0
 
     relay(1 - r)
     for d in range(1, 8):
         band(d).wait()
-    lower = split(li[...])
-    for j in range(4):
-        lanes = slice(128 * j, 128 * j + 128)
-        uf[:, lanes] = dot3(lower, split(m12[:, j].reshape(512, 128)))
-        uh[:, lanes], ul[:, lanes] = split(uf[:, lanes])
+    lih[...], lil[...] = split(li[...])
+    uih[...], uil[...] = split(ui[...])
+    prepare(0)
     left_of(1 - r)
     relay(r)
     lax.fori_loop(0, 4, finish, 0)
@@ -422,16 +476,19 @@
     def _():
         for d in range(1, 8):
             top(d).wait_send()
-        for d in range(1, 16):
-
-            @pl.when((g + d) % 16 != 0)
+        for p in range(1, 16):
+            part(p, 1).wait_send()
+
+            @pl.when(g != p % 8)
             def _():
-                part(d).wait_send()
-
-    @pl.when(g != 0)
-    def _():
-        for d in range(1, 8):
-            panel(d).wait_send()
+                part(p, 0).wait_send()
+
+    for e in range(2):
+
+        @pl.when(here + 8 * e != 0)
+        def _():
+            for d in range(1, 4):
+                panel(e, d).wait_send()
 
     for j in range(8):
 
@@ -461,8 +518,11 @@
         ((512, 512), f32),
         ((2, 512, 512), bf16),
         ((2, 512, 512), bf16),
-        ((2, 512, 512), f32),
         ((512, 512), f32),
+        ((512, 512), bf16),
+        ((512, 512), bf16),
+        ((512, 512), bf16),
+        ((512, 512), bf16),
         ((512, 512), bf16),
         ((512, 512), bf16),
         ((8, 2, 256, 128), f32),
@@ -473,7 +533,7 @@
         in_specs=[pl.BlockSpec(memory_space=pl.ANY), VMEM, VMEM],
         out_specs=VMEM,
         scratch_shapes=[pltpu.VMEM(*shape) for shape in shapes]
-        + [pltpu.SemaphoreType.DMA((14, 16))] * 2
+        + [pltpu.SemaphoreType.DMA((16, 16))] * 2
         + [pltpu.SemaphoreType.DMA((2,))],
         compiler_params=pltpu.CompilerParams(collective_id=0, has_side_effects=True),
         name="whole",

time: 113 us -> 109 us (0.965); the launches traced: 111 us -> 109 us
  Pallas kernels: 109 us -> 107 us
    pallas_call x1, Pallas kernels: 109 us -> 107 us  [shards(): pl.pallas_call(kernel, out_shape=pltpu.VMEM((2, 2048, 128), f32), in_spec...]
where the time goes in v4:
time: 109 us
  Pallas kernels  107 us (98%)
  local copies, waits for them, and re-layouts  1.32 us (1%)
    pallas_call x1, Pallas kernels, shards(): pl.pallas_call(kernel, out_shape=pltpu.VMEM((2, 2048, 128), f32), in_spec...  107 us

profile of v4, /device:TPU:6, one launch (start us, length us, event | category | flops | bytes accessed | tf_op | source)
XLA Modules:
  0.0 108.6 jit_solution(2641519436590201677)
XLA Ops:
  0.0 107.3 %whole.1 = f32[2,2048,128]{2,1,0:T(8,128)S(1)} custom-call(f32[2,2048,128]{2,1,0:T(8,128)} %bitcast.3, f32[2,4096]{1,0:T(2,128)} %rd.1, f32[2,128]{1,0:T(2,128)} %cd.1), custom_call_target="tpu_custom_call" | custom-call | tf_op jit(solution)/shard_map/whole/pallas_call | solution.py:530
  107.3 1.3 %copy.5 = f32[4096,128]{1,0:T(8,128)} copy(f32[4096,128]{1,0:T(8,128)S(1)} %bitcast.2) | data formatting | bytes 4194304

commit v5 on v4

--- a/solution.py
+++ b/solution.py
@@ -10,7 +10,7 @@
 MESH = pl.DeviceIdType.MESH
 VMEM = pl.BlockSpec(memory_space=pltpu.VMEM)
 GROUP = 4
-EARLY = (1, 2, 4, 6)
+EARLY = (1, 2, 3, 4, 5, 6, 7)
 
 
 def split(a):

time: 109 us -> 106 us (0.972)
  Pallas kernels: 107 us -> 104 us
    pallas_call x1, Pallas kernels: 107 us -> 104 us  [shards(): pl.pallas_call(kernel, out_shape=pltpu.VMEM((2, 2048, 128), f32), in_spec...]
where the time goes in v5:
time: 106 us
  Pallas kernels  104 us (98%)
  local copies, waits for them, and re-layouts  1.32 us (1%)
    pallas_call x1, Pallas kernels, shards(): pl.pallas_call(kernel, out_shape=pltpu.VMEM((2, 2048, 128), f32), in_spec...  104 us

profile of v5, /device:TPU:6, one launch (start us, length us, event | category | flops | bytes accessed | tf_op | source)
XLA Modules:
  0.0 105.6 jit_solution(1258603727495785919)
XLA Ops:
  0.0 104.3 %whole.1 = f32[2,2048,128]{2,1,0:T(8,128)S(1)} custom-call(f32[2,2048,128]{2,1,0:T(8,128)} %bitcast.3, f32[2,4096]{1,0:T(2,128)} %rd.1, f32[2,128]{1,0:T(2,128)} %cd.1), custom_call_target="tpu_custom_call" | custom-call | tf_op jit(solution)/shard_map/whole/pallas_call | solution.py:530
  104.3 1.3 %copy.5 = f32[4096,128]{1,0:T(8,128)} copy(f32[4096,128]{1,0:T(8,128)S(1)} %bitcast.2) | data formatting | bytes 4194304

commit v6 on v5

--- a/solution.py
+++ b/solution.py
@@ -251,8 +251,8 @@
         return remote(m21.at[p], m21.at[p], 11, j, j, partner)
 
     def target(slot):
-        half = slot // 4
-        return 4 * ((r + 1 + half) % 2) + (q + slot + half) % 4
+        half = slot % 2
+        return 4 * ((r + 1 + half) % 2) + (q + (slot + 1) // 2) % 4
 
     def back(slot, first):
         p = target(slot)
@@ -449,23 +449,22 @@
             back(slot, True).start()
             back(slot, False).start()
 
-        @pl.when(slot < 3)
-        def _():
-            prepare(slot + 1)
+        @pl.when((slot < 5) & (slot % 2 == 0))
+        def _():
+            prepare(slot // 2 + 1)
 
         return 0
 
     relay(1 - r)
+    relay(r)
     for d in range(1, 8):
         band(d).wait()
     lih[...], lil[...] = split(li[...])
     uih[...], uil[...] = split(ui[...])
     prepare(0)
     left_of(1 - r)
-    relay(r)
-    lax.fori_loop(0, 4, finish, 0)
     left_of(r)
-    lax.fori_loop(4, 8, finish, 0)
+    lax.fori_loop(0, 8, finish, 0)
     o[:, rows(m, 64)] = z[m, :, 0:64]
     o[:, rows(m, 192, 512)] = z[m, :, 64:256]
 

time: 106 us -> 105 us (level)
  no operation moved by 1% of the time
where the time goes in v6:
time: 105 us
  Pallas kernels  104 us (99%)
  local copies, waits for them, and re-layouts  1.32 us (1%)
    pallas_call x1, Pallas kernels, shards(): pl.pallas_call(kernel, out_shape=pltpu.VMEM((2, 2048, 128), f32), in_spec...  104 us

profile of v6, /device:TPU:6, one launch (start us, length us, event | category | flops | bytes accessed | tf_op | source)
XLA Modules:
  0.0 105.2 jit_solution(4395203394057554021)
XLA Ops:
  0.0 103.8 %whole.1 = f32[2,2048,128]{2,1,0:T(8,128)S(1)} custom-call(f32[2,2048,128]{2,1,0:T(8,128)} %bitcast.3, f32[2,4096]{1,0:T(2,128)} %rd.1, f32[2,128]{1,0:T(2,128)} %cd.1), custom_call_target="tpu_custom_call" | custom-call | tf_op jit(solution)/shard_map/whole/pallas_call | solution.py:529
  103.8 1.3 %copy.5 = f32[4096,128]{1,0:T(8,128)} copy(f32[4096,128]{1,0:T(8,128)S(1)} %bitcast.2) | data formatting | bytes 4194304
